TPU v7x, 256 devices: a whole 4x4x8 slice. The times are simulated.
256 devices in a mesh: gx: 4 (over y), gy: 16 (over z, core), gz: 4 (over x).
Axes of the slice: x: 4, y: 4, z: 8, core: 2. Of those that a mesh axis runs over, the one named last changes fastest.
Arguments:
- initial: float32 [256, 512, 1024], P('gx', 'gy', 'gz'), may hold values from -6 to 6
- right_side: float32 [256, 512, 1024], P('gx', 'gy', 'gz'), may hold values from -12 to 12
- shift_field: float32 [256, 512, 1024], P('gx', 'gy', 'gz'), may hold values from 0.5 to 8
Outputs:
- relaxed: float32 [256, 512, 1024], P('gx', 'gy', 'gz')
All inputs are finite; a program needn't handle non-finite values.
Results may differ from a plain program's by a relative error of at most 0.00002.
Values sent between devices are 32-bit elements; how exact they have to be, the bound alone decides.
No kernel may reach another device: no remote copies, remote signals or barrier semaphores. Data moves between devices by JAX's collectives and lax.ppermute only.
A program may use at most 128 MiB of HBM per device.

v0:
```python
import jax
import jax.numpy as jnp
from jax import lax
from jax.experimental import pallas as pl
from jax.experimental.pallas import tpu as pltpu
from jax.sharding import PartitionSpec as P


SWEEPS = 4
WIDE = 4
WEIGHT = 0.8
VMEM = pl.BlockSpec(memory_space=pltpu.VMEM)
HBM = pl.BlockSpec(memory_space=pltpu.HBM)
F32 = jnp.float32
CHUNK = 8
LAYERS = [(a, k) for a, n in enumerate((WIDE, WIDE - 1, WIDE - 1)) for k in range(n)]


def call(kernel, outs, operands, flops, scratch=(), limit=4, hbm_in=(), hbm_out=(), aliases={}):
    return pl.pallas_call(
        kernel,
        out_shape=[jax.ShapeDtypeStruct(s, F32) for s in outs],
        in_specs=[HBM if i in hbm_in else VMEM for i in range(len(operands))],
        out_specs=[HBM if i in hbm_out else VMEM for i in range(len(outs))],
        scratch_shapes=scratch,
        input_output_aliases=aliases,
        compiler_params=pltpu.CompilerParams(vmem_limit_bytes=limit * 2**20),
        cost_estimate=pl.CostEstimate(flops=flops, bytes_accessed=2**20, transcendentals=0),
    )(*operands)


def odd(axis):
    return lax.rem(lax.axis_index(axis), 2)


def swap(sent, axis):
    n = lax.axis_size(axis)
    near = [(i, i ^ 1) for i in range(n)]
    far = [(i, (i + (1 if i % 2 else -1)) % n) for i in range(n)]
    got = lax.ppermute(sent[1], axis, far)
    return lax.ppermute(sent[0], axis, near), got


def iota(shape, dim):
    return lax.broadcasted_iota(jnp.int32, shape, dim)


def fold(first, second, low):
    row = iota(first.shape, 0)
    keep = jnp.where(low, row, 7 - row) < 4
    return jnp.where(keep, first, pltpu.roll(second, 4, 0))


def unfold(above, below):
    head = iota(above.shape, 0) < 4
    return jnp.where(head, above, below), pltpu.roll(jnp.where(head, below, above), 4, 0)


def turn(tile, n):
    return pltpu.roll(tile, n % 8, 0) if n % 8 else tile


def fold_rows(held, x, at):
    row = iota((8, held[0].shape[2]), 0)
    tiles, rest = [], None
    for k in range(4):
        u, r, s = (ref[x + k, at : at + 8, :] for ref in held)
        if at == 0:
            tiles.append(jnp.where(row < 4, u, jnp.where(row < 7, turn(r, 4), turn(s, 7))))
            two = turn(s, 2 * k - 1)
        else:
            tiles.append(jnp.where(row > 3, u, jnp.where(row > 0, turn(r, 4), turn(s, 1))))
            two = turn(s, 2 * k - 5)
        rest = two if k == 0 else jnp.where(row // 2 == k, two, rest)
    return tiles + [rest]


def pack(u, r, s, u_v, r_v, s_v, y_near, y_far, z_near, z_far, x_near, x_far, sem):
    nx, ny, nz = u.shape
    y_odd, z_odd, x_odd = odd("gy") == 1, odd("gz") == 1, odd("gx") == 1
    held = (u_v, r_v, s_v)
    copies = {}
    for c in range(nx // CHUNK):
        at = pl.ds(c * CHUNK, CHUNK)
        for a, ref in enumerate((u, r, s)):
            copies[c, a] = pltpu.make_async_copy(ref.at[at], held[a].at[at], sem.at[c, a])
            copies[c, a].start()
    block = iota((ny, 128), 1) // 4
    half = iota((ny, 128), 1) < 64
    for c in range(nx // CHUNK):
        for a, ref in enumerate(held):
            copies[c, a].wait()
            g = c * CHUNK // 32
            first = c * CHUNK % 32 == 0
            low = jnp.zeros((ny, 128), F32) if first else z_near[a, g]
            high = jnp.zeros((ny, 128), F32) if first else z_far[a, g]
            low, high = jnp.where(z_odd, low, high), jnp.where(z_odd, high, low)
            for x in range(c * CHUNK, (c + 1) * CHUNK):
                j = x % 32
                both = jnp.where(half, ref[x, :, 0:128], ref[x, :, nz - 128 : nz])
                both = pltpu.roll(both, 4 * j, 1) if j else both
                low = jnp.where(block == j, both, low)
                high = jnp.where(block == (j - 1) % 32, both, high)
            z_near[a, g] = jnp.where(z_odd, low, high)
            z_far[a, g] = jnp.where(z_odd, high, low)
        for i in range(c * CHUNK // 4, (c + 1) * CHUNK // 4):
            low, high = fold_rows(held, 4 * i, 0), fold_rows(held, 4 * i, ny - 8)
            for n in range(5):
                y_near[i, n] = jnp.where(y_odd, low[n], high[n])
                y_far[i, n] = jnp.where(y_odd, high[n], low[n])
    for face, low in ((x_near, x_odd), (x_far, jnp.logical_not(x_odd))):
        for q, (a, k) in enumerate(LAYERS):
            layers = WIDE if a == 0 else WIDE - 1
            face[q] = held[a][jnp.where(low, k, nx - layers + k)]


def pack_yz(za, zb, near, far):
    ny = za.shape[2]
    is_odd = odd("gy") == 1
    for face, low in ((near, is_odd), (far, jnp.logical_not(is_odd))):
        rows = pl.ds(pl.multiple_of(jnp.where(low, 0, ny - 8), 8), 8)
        for a in range(3):
            for g in range(za.shape[1]):
                face[a, g] = fold(za[a, g, rows, :], zb[a, g, rows, :], low)


def weight(shift):
    return WEIGHT / (6.0 + shift)


def spread_z(high, low, j):
    tile = jnp.where(iota(high.shape, 1) // 4 == j, high, low)
    return pltpu.roll(tile, 128 - 4 * j, 1) if j else tile


def begin(u, r, s, w, part, edge):
    nx, ny, nz = u.shape
    row, lane = iota((ny, nz), 0), iota((ny, nz), 1)
    half = iota((ny, 128), 1) < 64

    def body(i, c):
        for j in range(8):
            x = 8 * i + j
            here = u[x]
            beside = u[jnp.maximum(x - 1, 0)] + u[jnp.minimum(x + 1, nx - 1)]
            beside = beside + jnp.where(row == 0, 0.0, pltpu.roll(here, 1, 0))
            beside = beside + jnp.where(row == ny - 1, 0.0, pltpu.roll(here, ny - 1, 0))
            left, right = pltpu.roll(here, 1, 1), pltpu.roll(here, nz - 1, 1)
            edge[x] = jnp.where(half, left[:, :128], right[:, nz - 128 :])
            beside = beside + (jnp.where(lane == 0, 0.0, left) + jnp.where(lane == nz - 1, 0.0, right))
            here_w = weight(s[x])
            w[x] = here_w
            part[x] = 0.2 * here + here_w * (r[x] + beside)
        return c

    lax.fori_loop(0, nx // 8, body, 0)


def finish(x, u0, r0, w0, part, edge, new):
    (u, yu, tu, eu), (_, yr, tr, er), (w, yw, tw, ew) = u0, r0, w0
    ny, nz = u.shape[1:]
    row, lane, lane_z = iota((8, nz), 0), iota((ny, 128), 1), iota((8, nz), 1)
    lane_e = iota((8, 128), 1)
    y, t, e = yu[x], tu[x], eu[x]
    t_left, t_right = pltpu.roll(t, 1, 1), pltpu.roll(t, 127, 1)
    e_left, e_right = pltpu.roll(e, 1, 1), pltpu.roll(e, 127, 1)
    y_left, y_right = pltpu.roll(y, 1, 1), pltpu.roll(y, nz - 1, 1)
    y_down, y_up = pltpu.roll(y, 1, 0), pltpu.roll(y, 7, 0)
    halo = jnp.concatenate([jnp.where(lane == 0, t_left, 0.0), jnp.where(lane == 127, t_right, 0.0)], 1)
    halo = jnp.concatenate(
        [
            halo[:8] + jnp.where(row == 0, y_down, 0.0),
            halo[8 : ny - 8],
            halo[ny - 8 :] + jnp.where(row == 7, y_up, 0.0),
        ],
        0,
    )
    new[x, :ny, :nz] = part[x] + w[x] * halo
    beside = yu[x - 1] + yu[x + 1]
    beside = beside + jnp.where(row == 0, pltpu.roll(u[x, ny - 8 :, :], 1, 0), y_down)
    beside = beside + jnp.where(row == 7, pltpu.roll(u[x, :8, :], 7, 0), y_up)
    left = jnp.where(lane_z == 0, jnp.concatenate([e_left, e_left], 1), y_left)
    right = jnp.where(lane_z == nz - 1, jnp.concatenate([e_right, e_right], 1), y_right)
    new[x, ny:, :nz] = 0.2 * y + yw[x] * (yr[x] + (beside + (left + right)))
    column = jnp.concatenate([t, e], 0)
    beside = jnp.concatenate([tu[x - 1] + tu[x + 1], eu[x - 1] + eu[x + 1]], 0)
    beside = beside + (pltpu.roll(column, 1, 0) + pltpu.roll(column, ny + 7, 0))
    left = [jnp.where(lane == 0, edge[x], t_left), jnp.where(lane_e == 0, y_left[:, :128], e_left)]
    right = [jnp.where(lane == 127, edge[x], t_right), jnp.where(lane_e == 127, y_right[:, nz - 128 :], e_right)]
    beside = beside + (jnp.concatenate(left, 0) + jnp.concatenate(right, 0))
    r, w = jnp.concatenate([tr[x], er[x]], 0), jnp.concatenate([tw[x], ew[x]], 0)
    new[x, :, nz:] = 0.2 * column + w * (r + beside)


def spread_z(high, low, j):
    tile = jnp.where(iota(high.shape, 1) // 4 == j, high, low)
    return pltpu.roll(tile, 128 - 4 * j, 1) if j else tile


def unpack_z(za, zb, tu, tr, tw):
    is_odd = odd("gz") == 1
    for a, out in enumerate((tu, tr, tw)):

        def body(g, c, a=a, out=out):
            one, two = za[a, g], zb[a, g]
            high, low = jnp.where(is_odd, two, one), jnp.where(is_odd, one, two)
            for j in range(32):
                tile = spread_z(high, low, j)
                out[g * 32 + j] = weight(tile) if a == 2 else tile
            return c

        lax.fori_loop(0, za.shape[1], body, 0)


def unpack_y(near, far, yu, yr, yw):
    is_odd = odd("gy") == 1
    row = iota(near.shape[2:], 0)

    def body(i, c):
        def halves(n):
            one, two = near[i, n], far[i, n]
            return jnp.where(is_odd, two, one), jnp.where(is_odd, one, two)

        rest_above, rest_below = halves(4)
        for k in range(4):
            above, below = halves(k)
            yu[4 * i + k] = jnp.where(row < 4, above, below)
            yr[4 * i + k] = turn(jnp.where(row < 4, below, above), 4)
            s = jnp.where(row < 4, turn(rest_above, 1 - 2 * k), turn(rest_below, 5 - 2 * k))
            s = jnp.where(row == 0, turn(above, 1), jnp.where(row == 7, turn(below, 7), s))
            yw[4 * i + k] = weight(s)
        return c

    lax.fori_loop(0, near.shape[0], body, 0, unroll=2)


def pack_edges(b_near, b_far, yu, yr, yw, tu, tr, tw, eu, er, ew, near, far):
    y_odd, z_odd, x_odd = odd("gy") == 1, odd("gz") == 1, odd("gx") == 1
    for a, out in enumerate((eu, er, ew)):
        for g in range(b_near.shape[1]):
            one, two = b_near[a, g], b_far[a, g]
            above, below = jnp.where(y_odd, two, one), jnp.where(y_odd, one, two)
            first, second = unfold(above, below)
            high, low = jnp.where(z_odd, second, first), jnp.where(z_odd, first, second)
            for j in range(32):
                tile = spread_z(high, low, j)
                out[g * 32 + j] = weight(tile) if a == 2 else tile
    nx = yu.shape[0]
    lane = iota((8, 128), 1) // 8
    for face, low in ((near, x_odd), (far, jnp.logical_not(x_odd))):
        total = [jnp.zeros((8, 128), F32)] * 5
        for q, (a, k) in enumerate(LAYERS):
            layers = WIDE if a == 0 else WIDE - 1
            x = jnp.where(low, k, nx - layers + k)
            face[q] = (yu, yr, yw)[a][x]
            for t in range(5):
                tile = (tu, tr, tw)[a][x, 8 * t : 8 * t + 8, :] if t < 4 else (eu, er, ew)[a][x]
                total[t] = jnp.where(lane == q, pltpu.roll(tile, 8 * q + 4, 1), total[t])
        for t in range(6):
            face[len(LAYERS) + t // 2, :, 128 * (t % 2) : 128 * (t % 2) + 128] = total[min(t, 4)]


def stencil(below, here, above, r, w):
    n, m = here.shape
    beside = below + above
    beside = beside + (pltpu.roll(here, 1, 0) + pltpu.roll(here, n - 1, 0))
    beside = beside + (pltpu.roll(here, 1, 1) + pltpu.roll(here, m - 1, 1))
    return 0.2 * here + w * (r + beside)


def final(below, here, above, r, w, ny, nz):
    row, lane = iota((8, nz), 0), iota((ny, 128), 1)
    tiles = [here[:ny, at : at + 128] for at in range(0, nz + 128, 128)]
    n = len(tiles)
    beside = below[:ny, :nz] + above[:ny, :nz]
    column = here[:, :nz]
    rows = column.shape[0]
    beside = beside + (pltpu.roll(column, 1, 0)[:ny] + pltpu.roll(column, rows - 1, 0)[:ny])
    left = [pltpu.roll(jnp.where(lane == 127, tiles[i - 1], tiles[i]), 1, 1) for i in range(n - 1)]
    right = [pltpu.roll(jnp.where(lane == 0, tiles[i + 1], tiles[i]), 127, 1) for i in range(n - 1)]
    beside = beside + (jnp.concatenate(left, 1) + jnp.concatenate(right, 1))
    return 0.2 * here[:ny, :nz] + w[:ny, :nz] * (r[:ny, :nz] + beside)


def whole(x, main, y, t, e):
    left = jnp.concatenate([main[x], y[x]], 0)
    return jnp.concatenate([left, jnp.concatenate([t[x], e[x]], 0)], 1)


PLANES = 4


def planes(i):
    return [(k, 1 + PLANES * i - k * (PLANES + 1) + j) for k in range(SWEEPS) for j in range(PLANES)]


def steps_of(nx):
    def valid(k, x):
        return k + 1 <= x <= nx - 2 - k

    count = -(-(nx - 1 + (SWEEPS - 1) * (PLANES + 1)) // PLANES)
    done = [[p for p in planes(i) if valid(*p)] for i in range(count)]
    full = [i for i in range(count) if len(done[i]) == SWEEPS * PLANES]
    first = planes(full[0])[-PLANES][1]
    stop = planes(full[-1])[-1][1] + 1
    return done, full, first, stop


def centre(*refs):
    u0, r0, w0 = refs[0:4], refs[4:8], refs[8:12]
    part, edge = refs[12:14]
    out, rest, ends = refs[14], refs[15], refs[16:19]
    last, sem = refs[19:21]
    steps = refs[21:24]
    nx, ny, nz = u0[0].shape
    done, full, first, stop = steps_of(nx)

    def plane(k, x):
        return steps[k - 1][x]

    def one(k, x):
        if k == 0:
            finish(x, u0, r0, w0, part, edge, steps[0])
            return
        r, w = whole(x, *r0), whole(x, *w0)
        near = plane(k, x - 1), plane(k, x), plane(k, x + 1)
        new = final(*near, r, w, ny, nz) if k == SWEEPS - 1 else stencil(*near, r, w)
        if k < SWEEPS - 2:
            steps[k][x] = new
        elif k == SWEEPS - 2:
            steps[k][x, :, :nz] = new[:, :nz]
            steps[k][x, :ny, nz:] = new[:ny, nz:]
        elif isinstance(x, int):
            rest[x - stop if x >= stop else nx - WIDE - stop + x - WIDE] = new
        else:
            last[x] = new

    for i in range(full[0]):
        for p in done[i]:
            one(*p)

    def body(i, c):
        for p in planes(i):
            one(*p)
        at = pl.ds(planes(i)[-PLANES][1], PLANES)
        pltpu.make_async_copy(last.at[at], out.at[at], sem).start()
        return c

    lax.fori_loop(full[0], full[-1] + 1, body, 0)
    for i in range(full[-1] + 1, len(done)):
        for p in done[i]:
            one(*p)
    for k in range(SWEEPS - 1):
        lo, hi = k + 1, nx - 1 - k
        for j, x in enumerate((lo, lo + 1, hi - 2, hi - 1)):
            ends[k][j] = steps[k][x]
    pltpu.make_async_copy(last.at[first:stop], out.at[first:stop], sem).wait()


def tail(*refs):
    u0, r0, w0 = refs[0:4], refs[4:8], refs[8:12]
    rest, ends = refs[13], refs[14:17]
    x_near, x_far, c_near, c_far = refs[17:21]
    out = refs[21]
    halo, last, sem = refs[22:25]
    steps = refs[25:28]
    nx, ny, nz = u0[0].shape
    _, _, first, stop = steps_of(nx)
    wait = []
    if first > WIDE:
        wait.append(pltpu.make_async_copy(rest.at[nx - WIDE - stop :], out.at[WIDE:first], sem.at[2]))
    wait.append(pltpu.make_async_copy(rest.at[: nx - WIDE - stop], out.at[stop : nx - WIDE], sem.at[3]))
    for copy in wait:
        copy.start()
    is_odd = odd("gx") == 1
    for side in (0, 1):
        flip = is_odd if side == 0 else jnp.logical_not(is_odd)
        for q, (a, k) in enumerate(LAYERS):
            main = jnp.where(flip, x_far[q], x_near[q])
            rows = jnp.where(flip, c_far[q], c_near[q])
            put = lambda v: weight(v) if a == 2 else v
            halo[side, q, :ny, :nz] = put(main)
            halo[side, q, ny:, :nz] = rows
            for t in range(5):
                at = (len(LAYERS) + t // 2, slice(None), slice(128 * (t % 2), 128 * (t % 2) + 128))
                tile = jnp.where(flip, c_far[at], c_near[at])
                halo[side, q, 8 * t : 8 * t + 8, nz:] = pltpu.roll(tile, 124 - 8 * q, 1)

    def start(a, x):
        layers = WIDE if a == 0 else WIDE - 1
        base = (0, WIDE, 2 * WIDE - 1)[a]
        if x >= nx:
            return halo[0, base + x - nx]
        if x < 0:
            return halo[1, base + layers + x]
        return whole(x, *(u0, r0, w0)[a])

    def span(side, k):
        return (nx - k, nx + SWEEPS - k) if side == 0 else (k - SWEEPS, k)

    def value(side, k, x):
        if k == 0:
            return start(0, x)
        for j, e in enumerate((k, k + 1, nx - 2 - k, nx - 1 - k)):
            if x == e:
                return ends[k - 1][j]
        return steps[k - 1][side, x - span(side, k)[0]]

    for k in range(1, SWEEPS + 1):
        for j in range(SWEEPS):
            for side in (0, 1):
                x = span(side, k)[0] + j
                near = [value(side, k - 1, x + d) for d in (-1, 0, 1)]
                coefficients = start(1, x), start(2, x)
                reach = SWEEPS - k - max(0, x - nx + 1, -x)
                if reach == 0:
                    new = final(*near, *coefficients, ny, nz)
                    if k == SWEEPS:
                        last[side, j] = new
                    else:
                        steps[k - 1][side, j, :ny, :nz] = new
                    continue
                new = stencil(*near, *coefficients)
                if reach > 1:
                    steps[k - 1][side, j] = new
                else:
                    steps[k - 1][side, j, :, :nz] = new[:, :nz]
                    steps[k - 1][side, j, :ny, nz:] = new[:ny, nz:]
    for side in (0, 1):
        a, b = span(side, SWEEPS)
        copy = pltpu.make_async_copy(last.at[side], out.at[a:b], sem.at[side])
        copy.start()
        wait.append(copy)
    for copy in wait:
        copy.wait()


def shards(u, r, s):
    nx, ny, nz = u.shape
    cells = nx * ny * nz
    raw = [pltpu.with_memory_space_constraint(v, pltpu.HBM) for v in (u, r, s)]
    faces = [(nx // 4, 5, 8, nz)] * 2 + [(3, nx // 32, ny, 128)] * 2 + [(len(LAYERS), ny, nz)] * 2
    scratch = [pltpu.SemaphoreType.DMA((nx // CHUNK, 3))]
    u, r, s, *sent = call(pack, [u.shape] * 3 + faces, raw, cells // 4, scratch, hbm_in=range(3))
    y = swap(sent[0:2], "gy")
    z = swap(sent[2:4], "gz")
    x = swap(sent[4:6], "gx")
    w, part, edge = call(begin, [u.shape] * 2 + [(nx, ny, 128)], (u, r, s), 20 * cells)
    sent = call(pack_yz, [(3, nx // 32, 8, 128)] * 2, z, cells // 64)
    b = swap(sent, "gy")
    t = call(unpack_z, [(nx, ny, 128)] * 3, z, 8 * cells)
    yy = call(unpack_y, [(nx, 8, nz)] * 3, y, cells)
    shape = (len(LAYERS) + 3, 8, nz)
    *e, c_near, c_far = call(pack_edges, [(nx, 8, 128)] * 3 + [shape] * 2, (*b, *yy, *t), cells // 8)
    c = swap((c_near, c_far), "gx")
    parts = [v for a, m in enumerate((u, r, w)) for v in (m, yy[a], t[a], e[a])]
    block = (ny + 2 * WIDE, nz + 128)
    _, _, first, stop = steps_of(nx)
    scratch = [pltpu.VMEM(u.shape, F32), pltpu.SemaphoreType.DMA] + [pltpu.VMEM((nx,) + block, F32)] * 3
    left = (nx - WIDE - stop + first - WIDE, ny, nz)
    out, rest, *ends = call(
        centre, [u.shape, left] + [(4,) + block] * 3, (*parts, part, edge), 60 * cells, scratch, 16, hbm_out=(0,)
    )
    scratch = [
        pltpu.VMEM((2, len(LAYERS)) + block, F32),
        pltpu.VMEM((2, WIDE, ny, nz), F32),
        pltpu.SemaphoreType.DMA((4,)),
    ] + [pltpu.VMEM((2, SWEEPS) + block, F32)] * 3
    operands = (*parts, out, rest, *ends, *x, *c)
    (out,) = call(
        tail, [u.shape], operands, 8 * cells, scratch, 8, hbm_in=(12,), hbm_out=(0,), aliases={12: 0}
    )
    return out


def solution(mesh):
    spec = P("gx", "gy", "gz")
    return jax.shard_map(shards, mesh=mesh, in_specs=(spec,) * 3, out_specs=spec, check_vma=False)
```

profile of v0, /device:TPU:1, one launch (start us, length us, event | category | flops | bytes accessed | tf_op | source)
XLA Modules:
  0.0 40.0 jit_solution(373488941092432424)
XLA Ops:
  0.0 3.9 %shard_map.37 = (f32[64,32,256]{2,1,0:T(8,128)S(1)}, f32[64,32,256]{2,1,0:T(8,128)S(1)}, f32[64,32,256]{2,1,0:T(8,128)S(1)}, f32[16,5,8,256]{3,2,1,0:T(8,128)S(1...) custom-call(f32[64,32,256]{2,1,0:T(8,128)} %u.1, ...), custom_call_target="tpu_custom_call" | custom-call | flops 131072 | bytes 1048576 | tf_op jit(solution)/shard_map/pallas_call | solution.py:20
  3.9 3.3 %collective-permute-start = (f32[16,5,8,256]{3,2,1,0:T(8,128)S(1)}, f32[16,5,8,256]{3,2,1,0:T(8,128)S(1)}, u32[]{:S(2)}, u32[]{:S(2)}) collective-permute-start(f32[16,5,8,256]{3,2,1,0:T(8,128)S(1)} %get-tuple-element.36), channel_id=1, source_target_pairs={{0,4},{4,0},{8,12},{12,8},{16,20},{20,16},{24,28},{28,24},{32,36},... | collective-permute-start | bytes 1966088 | tf_op jit(solution)/shard_map/ppermute | solution.py:41
  7.2 0.0 collective-permute-start.1
  7.2 1.1 %collective-permute-start.2 = (f32[3,2,32,128]{3,2,1,0:T(8,128)S(1)}, f32[3,2,32,128]{3,2,1,0:T(8,128)S(1)}, u32[]{:S(2)}, u32[]{:S(2)}) collective-permute-start(f32[3,2,32,128]{3,2,1,0:T(8,128)S(1)} %get-tuple-element.39), channel_id=1, source_target_pairs={{0,1},{1,0},{2,3},{3,2},{4,5},{5,4},{6,7},{7,6},{8,9},{9,8},{10,11... | collective-permute-start | bytes 294920 | tf_op jit(solution)/shard_map/ppermute | solution.py:41
  8.4 1.3 %collective-permute-start.6 = (f32[10,32,256]{2,1,0:T(8,128)S(1)}, f32[10,32,256]{2,1,0:T(8,128)S(1)}, u32[]{:S(2)}, u32[]{:S(2)}) collective-permute-start(f32[10,32,256]{2,1,0:T(8,128)S(1)} %get-tuple-element.61), channel_id=1, source_target_pairs={{0,64},{64,0},{128,192},{192,128},{1,65},{65,1},{129,193},{193,129... | collective-permute-start | bytes 983048 | tf_op jit(solution)/shard_map/ppermute | solution.py:41
  9.7 1.9 %collective-permute-start.7 = (f32[10,32,256]{2,1,0:T(8,128)S(1)}, f32[10,32,256]{2,1,0:T(8,128)S(1)}, u32[]{:S(2)}, u32[]{:S(2)}) collective-permute-start(f32[10,32,256]{2,1,0:T(8,128)S(1)} %get-tuple-element.62), channel_id=1, source_target_pairs={{0,192},{64,128},{128,64},{192,0},{1,193},{65,129},{129,65},{193,1... | collective-permute-start | bytes 983048 | tf_op jit(solution)/shard_map/ppermute | solution.py:40
  11.6 0.0 collective-permute-done.2.za
  11.6 1.8 %collective-permute-start.3 = (f32[3,2,32,128]{3,2,1,0:T(8,128)S(1)}, f32[3,2,32,128]{3,2,1,0:T(8,128)S(1)}, u32[]{:S(2)}, u32[]{:S(2)}) collective-permute-start(f32[3,2,32,128]{3,2,1,0:T(8,128)S(1)} %get-tuple-element.40), channel_id=1, source_target_pairs={{0,3},{1,2},{2,1},{3,0},{4,7},{5,6},{6,5},{7,4},{8,11},{9,10},{10,... | collective-permute-start | bytes 294920 | tf_op jit(solution)/shard_map/ppermute | solution.py:40
  13.4 3.2 %collective-permute-done.3.zb = f32[3,2,32,128]{3,2,1,0:T(8,128)S(1)} collective-permute-done((f32[3,2,32,128]{3,2,1,0:T(8,128)S(1)}, f32[3,2,32,128]{3,2,1,0:T(8,128)S(1)}, u32[]{:S(2)}, u32[]{:S(2)}) %collective-permute-start.3) | collective-permute-done | bytes 98336 | tf_op jit(solution)/shard_map/ppermute | solution.py:40
  16.6 6.1 %collective-permute-start.4 = (f32[3,2,8,128]{3,2,1,0:T(8,128)S(1)}, f32[3,2,8,128]{3,2,1,0:T(8,128)S(1)}, u32[]{:S(2)}, u32[]{:S(2)}) collective-permute-start(f32[3,2,8,128]{3,2,1,0:T(8,128)S(1)} %get-tuple-element.42), channel_id=1, source_target_pairs={{0,4},{4,0},{8,12},{12,8},{16,20},{20,16},{24,28},{28,24},{32,36},... | collective-permute-start | bytes 73736 | tf_op jit(solution)/shard_map/ppermute | solution.py:41
  22.7 0.0 collective-permute-done.near
  22.7 0.0 collective-permute-start.5
  22.7 1.2 %shard_map.39 = (f32[64,32,128]{2,1,0:T(8,128)S(1)}, f32[64,32,128]{2,1,0:T(8,128)S(1)}, f32[64,32,128]{2,1,0:T(8,128)S(1)}) custom-call(f32[3,2,32,128]{3,2,1,0:T(8,128)S(1)} %collective-permute-done.2.za, f32[3,2,32,128]{3,2,1,0:T(8,128)S(1)} %collective-permute-done.3.zb), custom_call_target="tpu_custom_call" | custom-call | flops 4194304 | bytes 1048576 | tf_op jit(solution)/shard_map/pallas_call | solution.py:20
  23.9 0.0 collective-permute-done.1.far
  23.9 0.4 shard_map.38
  24.3 0.0 collective-permute-done.4.b_near
  24.3 1.6 %collective-permute-done.5.b_far = f32[3,2,8,128]{3,2,1,0:T(8,128)S(1)} collective-permute-done((f32[3,2,8,128]{3,2,1,0:T(8,128)S(1)}, f32[3,2,8,128]{3,2,1,0:T(8,128)S(1)}, u32[]{:S(2)}, u32[]{:S(2)}) %collective-permute-start.5) | collective-permute-done | bytes 24608 | tf_op jit(solution)/shard_map/ppermute | solution.py:40
  25.9 0.4 %shard_map.41 = (f32[64,8,128]{2,1,0:T(8,128)S(1)}, f32[64,8,128]{2,1,0:T(8,128)S(1)}, f32[64,8,128]{2,1,0:T(8,128)S(1)}, f32[13,8,256]{2,1,0:T(8,128)S(1)}, f32[13,8,256]{2,1,0:T(8,128)S(1)}) custom-call(f32[3,2,8,128]{3,2,1,0:T(8,128)S(1)} %collective-permute-done.4.b_near, f32[3,2,8,128]{3,2,1,0:T(8,128)S(1)} %collective-permute-done.5.b_far, ...), custom_call_target="tpu_custom_call" | custom-call | flops 65536 | bytes 1048576 | tf_op jit(solution)/shard_map/pallas_call | solution.py:20
  26.4 0.7 %collective-permute-start.8 = (f32[13,8,256]{2,1,0:T(8,128)S(1)}, f32[13,8,256]{2,1,0:T(8,128)S(1)}, u32[]{:S(2)}, u32[]{:S(2)}) collective-permute-start(f32[13,8,256]{2,1,0:T(8,128)S(1)} %get-tuple-element.63), channel_id=1, source_target_pairs={{0,64},{64,0},{128,192},{192,128},{1,65},{65,1},{129,193},{193,129... | collective-permute-start | bytes 319496 | tf_op jit(solution)/shard_map/ppermute | solution.py:41
  27.1 1.9 %collective-permute-start.9 = (f32[13,8,256]{2,1,0:T(8,128)S(1)}, f32[13,8,256]{2,1,0:T(8,128)S(1)}, u32[]{:S(2)}, u32[]{:S(2)}) collective-permute-start(f32[13,8,256]{2,1,0:T(8,128)S(1)} %get-tuple-element.64), channel_id=1, source_target_pairs={{0,192},{64,128},{128,64},{192,0},{1,193},{65,129},{129,65},{193,1... | collective-permute-start | bytes 319496 | tf_op jit(solution)/shard_map/ppermute | solution.py:40
  29.0 1.9 %shard_map.42 = (f32[64,32,256]{2,1,0:T(8,128)S(1)}, f32[64,32,256]{2,1,0:T(8,128)S(1)}, f32[64,32,128]{2,1,0:T(8,128)S(1)}) custom-call(f32[64,32,256]{2,1,0:T(8,128)S(1)} %get-tuple-element.35.u.refs_0_, f32[64,32,256]{2,1,0:T(8,128)S(1)} %get-tuple-element.49.r.refs_4_, f32[64,32,256]{2,1,0:T(8,128)S(1)} %get-tuple-element.51.s), custom_call_target="tpu_custom_call" | custom-call | flops 10485760 | bytes 1048576 | tf_op jit(solution)/shard_map/pallas_call | solution.py:20
  30.9 7.1 %shard_map.43 = (f32[64,32,256]{2,1,0:T(8,128)}, f32[16,32,256]{2,1,0:T(8,128)S(1)}, f32[4,40,384]{2,1,0:T(8,128)S(1)}, f32[4,40,384]{2,1,0:T(8,128)S(1)}, f32[4,40,384]{2,1,0:T(8,128)S(1)}) custom-call(f32[64,32,256]{2,1,0:T(8,128)S(1)} %get-tuple-element.35.u.refs_0_, f32[64,8,256]{2,1,0:T(8,128)S(1)} %get-tuple-element.38.yu.refs_1_, ...), custom_call_target="tpu_custom_call" | custom-call | flops 31457280 | bytes 1048576 | tf_op jit(solution)/shard_map/pallas_call | solution.py:20
  38.0 0.0 collective-permute-done.6.refs_17_
  38.0 0.0 collective-permute-done.7.refs_18_
  38.0 0.0 collective-permute-done.8.refs_19_
  38.0 0.0 collective-permute-done.9.refs_20_
  38.0 1.9 %shard_map.44 = f32[64,32,256]{2,1,0:T(8,128)} custom-call(f32[64,32,256]{2,1,0:T(8,128)S(1)} %get-tuple-element.35.u.refs_0_, f32[64,8,256]{2,1,0:T(8,128)S(1)} %get-tuple-element.38.yu.refs_1_, f32[64,32,128]{2,1,0:T(8,128)S(1)} %get-tuple-element.41.tu.refs_2_, f32[64,8,128]{2,1,0:T(8,128)S(1)} %get-tuple-element.48.refs_3_, ...), custom_call_target="tpu_custom_call", output_to_operand_aliasing={{}: (12, {})} | custom-call | flops 4194304 | bytes 1048576 | tf_op jit(solution)/shard_map/pallas_call | solution.py:20
  (1 shorter events, 0.0 us)
Async XLA Ops:
  3.9 18.7 %collective-permute-start = (f32[16,5,8,256]{3,2,1,0:T(8,128)S(1)}, f32[16,5,8,256]{3,2,1,0:T(8,128)S(1)}, u32[]{:S(2)}, u32[]{:S(2)}) collective-permute-start(f32[16,5,8,256]{3,2,1,0:T(8,128)S(1)} %get-tuple-element.36), channel_id=1, source_target_pairs={{0,4},{4,0},{8,12},{12,8},{16,20},{20,16},{24,28},{28,24},{32,36},... | collective-permute-start | bytes 1966088 | tf_op jit(solution)/shard_map/ppermute | solution.py:41
  7.2 16.7 %collective-permute-start.1 = (f32[16,5,8,256]{3,2,1,0:T(8,128)S(1)}, f32[16,5,8,256]{3,2,1,0:T(8,128)S(1)}, u32[]{:S(2)}, u32[]{:S(2)}) collective-permute-start(f32[16,5,8,256]{3,2,1,0:T(8,128)S(1)} %get-tuple-element.37), channel_id=1, source_target_pairs={{0,60},{4,8},{8,4},{12,16},{16,12},{20,24},{24,20},{28,32},{32,28}... | collective-permute-start | bytes 1966088 | tf_op jit(solution)/shard_map/ppermute | solution.py:40
  7.2 4.3 %collective-permute-start.2 = (f32[3,2,32,128]{3,2,1,0:T(8,128)S(1)}, f32[3,2,32,128]{3,2,1,0:T(8,128)S(1)}, u32[]{:S(2)}, u32[]{:S(2)}) collective-permute-start(f32[3,2,32,128]{3,2,1,0:T(8,128)S(1)} %get-tuple-element.39), channel_id=1, source_target_pairs={{0,1},{1,0},{2,3},{3,2},{4,5},{5,4},{6,7},{7,6},{8,9},{9,8},{10,11... | collective-permute-start | bytes 294920 | tf_op jit(solution)/shard_map/ppermute | solution.py:41
  8.4 29.6 %collective-permute-start.6 = (f32[10,32,256]{2,1,0:T(8,128)S(1)}, f32[10,32,256]{2,1,0:T(8,128)S(1)}, u32[]{:S(2)}, u32[]{:S(2)}) collective-permute-start(f32[10,32,256]{2,1,0:T(8,128)S(1)} %get-tuple-element.61), channel_id=1, source_target_pairs={{0,64},{64,0},{128,192},{192,128},{1,65},{65,1},{129,193},{193,129... | collective-permute-start | bytes 983048 | tf_op jit(solution)/shard_map/ppermute | solution.py:41
  9.7 28.3 %collective-permute-start.7 = (f32[10,32,256]{2,1,0:T(8,128)S(1)}, f32[10,32,256]{2,1,0:T(8,128)S(1)}, u32[]{:S(2)}, u32[]{:S(2)}) collective-permute-start(f32[10,32,256]{2,1,0:T(8,128)S(1)} %get-tuple-element.62), channel_id=1, source_target_pairs={{0,192},{64,128},{128,64},{192,0},{1,193},{65,129},{129,65},{193,1... | collective-permute-start | bytes 983048 | tf_op jit(solution)/shard_map/ppermute | solution.py:40
  11.6 5.0 %collective-permute-start.3 = (f32[3,2,32,128]{3,2,1,0:T(8,128)S(1)}, f32[3,2,32,128]{3,2,1,0:T(8,128)S(1)}, u32[]{:S(2)}, u32[]{:S(2)}) collective-permute-start(f32[3,2,32,128]{3,2,1,0:T(8,128)S(1)} %get-tuple-element.40), channel_id=1, source_target_pairs={{0,3},{1,2},{2,1},{3,0},{4,7},{5,6},{6,5},{7,4},{8,11},{9,10},{10,... | collective-permute-start | bytes 294920 | tf_op jit(solution)/shard_map/ppermute | solution.py:40
  16.6 7.7 %collective-permute-start.4 = (f32[3,2,8,128]{3,2,1,0:T(8,128)S(1)}, f32[3,2,8,128]{3,2,1,0:T(8,128)S(1)}, u32[]{:S(2)}, u32[]{:S(2)}) collective-permute-start(f32[3,2,8,128]{3,2,1,0:T(8,128)S(1)} %get-tuple-element.42), channel_id=1, source_target_pairs={{0,4},{4,0},{8,12},{12,8},{16,20},{20,16},{24,28},{28,24},{32,36},... | collective-permute-start | bytes 73736 | tf_op jit(solution)/shard_map/ppermute | solution.py:41
  22.7 3.3 %collective-permute-start.5 = (f32[3,2,8,128]{3,2,1,0:T(8,128)S(1)}, f32[3,2,8,128]{3,2,1,0:T(8,128)S(1)}, u32[]{:S(2)}, u32[]{:S(2)}) collective-permute-start(f32[3,2,8,128]{3,2,1,0:T(8,128)S(1)} %get-tuple-element.43), channel_id=1, source_target_pairs={{0,60},{4,8},{8,4},{12,16},{16,12},{20,24},{24,20},{28,32},{32,28}... | collective-permute-start | bytes 73736 | tf_op jit(solution)/shard_map/ppermute | solution.py:40
  26.4 11.6 %collective-permute-start.8 = (f32[13,8,256]{2,1,0:T(8,128)S(1)}, f32[13,8,256]{2,1,0:T(8,128)S(1)}, u32[]{:S(2)}, u32[]{:S(2)}) collective-permute-start(f32[13,8,256]{2,1,0:T(8,128)S(1)} %get-tuple-element.63), channel_id=1, source_target_pairs={{0,64},{64,0},{128,192},{192,128},{1,65},{65,1},{129,193},{193,129... | collective-permute-start | bytes 319496 | tf_op jit(solution)/shard_map/ppermute | solution.py:41
  27.1 10.9 %collective-permute-start.9 = (f32[13,8,256]{2,1,0:T(8,128)S(1)}, f32[13,8,256]{2,1,0:T(8,128)S(1)}, u32[]{:S(2)}, u32[]{:S(2)}) collective-permute-start(f32[13,8,256]{2,1,0:T(8,128)S(1)} %get-tuple-element.64), channel_id=1, source_target_pairs={{0,192},{64,128},{128,64},{192,0},{1,193},{65,129},{129,65},{193,1... | collective-permute-start | bytes 319496 | tf_op jit(solution)/shard_map/ppermute | solution.py:40
where the time goes:
time: 40.5 us; the launch traced here: 40 us
  starting transfers between devices  18.2 us (45%)
  Pallas kernels  16.8 us (41%)
  waiting for transfers between devices  4.81 us (12%)
    pallas_call x8, Pallas kernels, call(): pl.pallas_call(kernel, out_shape=[jax.ShapeDtypeStruct(s, F32) for s in o...  16.8 us
    ppermute x5, starting transfers between devices, swap(): return (lax.ppermute(sent[0], axis, near), got)  12.6 us
    ppermute x5, starting transfers between devices, swap(): got = lax.ppermute(sent[1], axis, far)  5.63 us
    ppermute x5, waiting for transfers between devices, swap(): got = lax.ppermute(sent[1], axis, far)  4.8 us
  transfers between devices with their start and end apart: 10, of which 2 were waited for; matrix products, arithmetic and copies ran while one was open for 0% of the time, Pallas kernels for 27%

commit v1 on v0

--- a/solution.py
+++ b/solution.py
@@ -12,7 +12,6 @@
 VMEM = pl.BlockSpec(memory_space=pltpu.VMEM)
 HBM = pl.BlockSpec(memory_space=pltpu.HBM)
 F32 = jnp.float32
-CHUNK = 8
 LAYERS = [(a, k) for a, n in enumerate((WIDE, WIDE - 1, WIDE - 1)) for k in range(n)]
 
 
@@ -54,6 +53,11 @@
 def unfold(above, below):
     head = iota(above.shape, 0) < 4
     return jnp.where(head, above, below), pltpu.roll(jnp.where(head, below, above), 4, 0)
+
+
+def chunks(nx):
+    sizes = [32] * (nx // 32 - 1) + [16, 16]
+    return [(sum(sizes[:i]), n) for i, n in enumerate(sizes)]
 
 
 def turn(tile, n):
@@ -80,22 +84,22 @@
     y_odd, z_odd, x_odd = odd("gy") == 1, odd("gz") == 1, odd("gx") == 1
     held = (u_v, r_v, s_v)
     copies = {}
-    for c in range(nx // CHUNK):
-        at = pl.ds(c * CHUNK, CHUNK)
+    for c, (x0, size) in enumerate(chunks(nx)):
+        at = pl.ds(x0, size)
         for a, ref in enumerate((u, r, s)):
             copies[c, a] = pltpu.make_async_copy(ref.at[at], held[a].at[at], sem.at[c, a])
             copies[c, a].start()
     block = iota((ny, 128), 1) // 4
     half = iota((ny, 128), 1) < 64
-    for c in range(nx // CHUNK):
+    for c, (x0, size) in enumerate(chunks(nx)):
         for a, ref in enumerate(held):
             copies[c, a].wait()
-            g = c * CHUNK // 32
-            first = c * CHUNK % 32 == 0
+            g = x0 // 32
+            first = x0 % 32 == 0
             low = jnp.zeros((ny, 128), F32) if first else z_near[a, g]
             high = jnp.zeros((ny, 128), F32) if first else z_far[a, g]
             low, high = jnp.where(z_odd, low, high), jnp.where(z_odd, high, low)
-            for x in range(c * CHUNK, (c + 1) * CHUNK):
+            for x in range(x0, x0 + size):
                 j = x % 32
                 both = jnp.where(half, ref[x, :, 0:128], ref[x, :, nz - 128 : nz])
                 both = pltpu.roll(both, 4 * j, 1) if j else both
@@ -103,7 +107,7 @@
                 high = jnp.where(block == (j - 1) % 32, both, high)
             z_near[a, g] = jnp.where(z_odd, low, high)
             z_far[a, g] = jnp.where(z_odd, high, low)
-        for i in range(c * CHUNK // 4, (c + 1) * CHUNK // 4):
+        for i in range(x0 // 4, (x0 + size) // 4):
             low, high = fold_rows(held, 4 * i, 0), fold_rows(held, 4 * i, ny - 8)
             for n in range(5):
                 y_near[i, n] = jnp.where(y_odd, low[n], high[n])
@@ -440,7 +444,7 @@
     cells = nx * ny * nz
     raw = [pltpu.with_memory_space_constraint(v, pltpu.HBM) for v in (u, r, s)]
     faces = [(nx // 4, 5, 8, nz)] * 2 + [(3, nx // 32, ny, 128)] * 2 + [(len(LAYERS), ny, nz)] * 2
-    scratch = [pltpu.SemaphoreType.DMA((nx // CHUNK, 3))]
+    scratch = [pltpu.SemaphoreType.DMA((len(chunks(nx)), 3))]
     u, r, s, *sent = call(pack, [u.shape] * 3 + faces, raw, cells // 4, scratch, hbm_in=range(3))
     y = swap(sent[0:2], "gy")
     z = swap(sent[2:4], "gz")

time: 40.5 us -> 39.8 us (0.983)
  Pallas kernels: 16.8 us -> 16.1 us
    pallas_call x8, Pallas kernels: 16.8 us -> 16.1 us  [call(): pl.pallas_call(kernel, out_shape=[jax.ShapeDtypeStruct(s, F32) for s in o...]
  transfers between devices with their start and end apart: 10 -> 10, of which waited for: 2 -> 2; matrix products, arithmetic and copies ran while one was open for 0% -> 0% of each run, Pallas kernels for 27% -> 28%
where the time goes in v1:
time: 39.8 us; the launch traced here: 39.4 us
  starting transfers between devices  18.2 us (46%)
  Pallas kernels  16.1 us (40%)
  waiting for transfers between devices  4.81 us (12%)
    pallas_call x8, Pallas kernels, call(): pl.pallas_call(kernel, out_shape=[jax.ShapeDtypeStruct(s, F32) for s in o...  16.1 us
    ppermute x5, starting transfers between devices, swap(): return (lax.ppermute(sent[0], axis, near), got)  12.6 us
    ppermute x5, starting transfers between devices, swap(): got = lax.ppermute(sent[1], axis, far)  5.63 us
    ppermute x5, waiting for transfers between devices, swap(): got = lax.ppermute(sent[1], axis, far)  4.8 us
  transfers between devices with their start and end apart: 10, of which 2 were waited for; matrix products, arithmetic and copies ran while one was open for 0% of the time, Pallas kernels for 28%

profile of v1, /device:TPU:1, one launch (start us, length us, event | category | flops | bytes accessed | tf_op | source)
XLA Modules:
  0.0 39.4 jit_solution(13347779628758638521)
XLA Ops:
  0.0 3.3 %shard_map.37 = (f32[64,32,256]{2,1,0:T(8,128)S(1)}, f32[64,32,256]{2,1,0:T(8,128)S(1)}, f32[64,32,256]{2,1,0:T(8,128)S(1)}, f32[16,5,8,256]{3,2,1,0:T(8,128)S(1...) custom-call(f32[64,32,256]{2,1,0:T(8,128)} %u.1, ...), custom_call_target="tpu_custom_call" | custom-call | flops 131072 | bytes 1048576 | tf_op jit(solution)/shard_map/pallas_call | solution.py:19
  3.3 3.3 %collective-permute-start = (f32[16,5,8,256]{3,2,1,0:T(8,128)S(1)}, f32[16,5,8,256]{3,2,1,0:T(8,128)S(1)}, u32[]{:S(2)}, u32[]{:S(2)}) collective-permute-start(f32[16,5,8,256]{3,2,1,0:T(8,128)S(1)} %get-tuple-element.36), channel_id=1, source_target_pairs={{0,4},{4,0},{8,12},{12,8},{16,20},{20,16},{24,28},{28,24},{32,36},... | collective-permute-start | bytes 1966088 | tf_op jit(solution)/shard_map/ppermute | solution.py:40
  6.6 0.0 collective-permute-start.1
  6.6 1.1 %collective-permute-start.2 = (f32[3,2,32,128]{3,2,1,0:T(8,128)S(1)}, f32[3,2,32,128]{3,2,1,0:T(8,128)S(1)}, u32[]{:S(2)}, u32[]{:S(2)}) collective-permute-start(f32[3,2,32,128]{3,2,1,0:T(8,128)S(1)} %get-tuple-element.39), channel_id=1, source_target_pairs={{0,1},{1,0},{2,3},{3,2},{4,5},{5,4},{6,7},{7,6},{8,9},{9,8},{10,11... | collective-permute-start | bytes 294920 | tf_op jit(solution)/shard_map/ppermute | solution.py:40
  7.7 1.3 %collective-permute-start.6 = (f32[10,32,256]{2,1,0:T(8,128)S(1)}, f32[10,32,256]{2,1,0:T(8,128)S(1)}, u32[]{:S(2)}, u32[]{:S(2)}) collective-permute-start(f32[10,32,256]{2,1,0:T(8,128)S(1)} %get-tuple-element.61), channel_id=1, source_target_pairs={{0,64},{64,0},{128,192},{192,128},{1,65},{65,1},{129,193},{193,129... | collective-permute-start | bytes 983048 | tf_op jit(solution)/shard_map/ppermute | solution.py:40
  9.0 1.9 %collective-permute-start.7 = (f32[10,32,256]{2,1,0:T(8,128)S(1)}, f32[10,32,256]{2,1,0:T(8,128)S(1)}, u32[]{:S(2)}, u32[]{:S(2)}) collective-permute-start(f32[10,32,256]{2,1,0:T(8,128)S(1)} %get-tuple-element.62), channel_id=1, source_target_pairs={{0,192},{64,128},{128,64},{192,0},{1,193},{65,129},{129,65},{193,1... | collective-permute-start | bytes 983048 | tf_op jit(solution)/shard_map/ppermute | solution.py:39
  10.9 0.0 collective-permute-done.2.za
  10.9 1.8 %collective-permute-start.3 = (f32[3,2,32,128]{3,2,1,0:T(8,128)S(1)}, f32[3,2,32,128]{3,2,1,0:T(8,128)S(1)}, u32[]{:S(2)}, u32[]{:S(2)}) collective-permute-start(f32[3,2,32,128]{3,2,1,0:T(8,128)S(1)} %get-tuple-element.40), channel_id=1, source_target_pairs={{0,3},{1,2},{2,1},{3,0},{4,7},{5,6},{6,5},{7,4},{8,11},{9,10},{10,... | collective-permute-start | bytes 294920 | tf_op jit(solution)/shard_map/ppermute | solution.py:39
  12.7 3.2 %collective-permute-done.3.zb = f32[3,2,32,128]{3,2,1,0:T(8,128)S(1)} collective-permute-done((f32[3,2,32,128]{3,2,1,0:T(8,128)S(1)}, f32[3,2,32,128]{3,2,1,0:T(8,128)S(1)}, u32[]{:S(2)}, u32[]{:S(2)}) %collective-permute-start.3) | collective-permute-done | bytes 98336 | tf_op jit(solution)/shard_map/ppermute | solution.py:39
  15.9 6.1 %collective-permute-start.4 = (f32[3,2,8,128]{3,2,1,0:T(8,128)S(1)}, f32[3,2,8,128]{3,2,1,0:T(8,128)S(1)}, u32[]{:S(2)}, u32[]{:S(2)}) collective-permute-start(f32[3,2,8,128]{3,2,1,0:T(8,128)S(1)} %get-tuple-element.42), channel_id=1, source_target_pairs={{0,4},{4,0},{8,12},{12,8},{16,20},{20,16},{24,28},{28,24},{32,36},... | collective-permute-start | bytes 73736 | tf_op jit(solution)/shard_map/ppermute | solution.py:40
  22.0 0.0 collective-permute-done.near
  22.0 0.0 collective-permute-start.5
  22.0 1.2 %shard_map.39 = (f32[64,32,128]{2,1,0:T(8,128)S(1)}, f32[64,32,128]{2,1,0:T(8,128)S(1)}, f32[64,32,128]{2,1,0:T(8,128)S(1)}) custom-call(f32[3,2,32,128]{3,2,1,0:T(8,128)S(1)} %collective-permute-done.2.za, f32[3,2,32,128]{3,2,1,0:T(8,128)S(1)} %collective-permute-done.3.zb), custom_call_target="tpu_custom_call" | custom-call | flops 4194304 | bytes 1048576 | tf_op jit(solution)/shard_map/pallas_call | solution.py:19
  23.3 0.0 collective-permute-done.1.far
  23.3 0.4 shard_map.38
  23.6 0.0 collective-permute-done.4.b_near
  23.7 1.6 %collective-permute-done.5.b_far = f32[3,2,8,128]{3,2,1,0:T(8,128)S(1)} collective-permute-done((f32[3,2,8,128]{3,2,1,0:T(8,128)S(1)}, f32[3,2,8,128]{3,2,1,0:T(8,128)S(1)}, u32[]{:S(2)}, u32[]{:S(2)}) %collective-permute-start.5) | collective-permute-done | bytes 24608 | tf_op jit(solution)/shard_map/ppermute | solution.py:39
  25.3 0.4 %shard_map.41 = (f32[64,8,128]{2,1,0:T(8,128)S(1)}, f32[64,8,128]{2,1,0:T(8,128)S(1)}, f32[64,8,128]{2,1,0:T(8,128)S(1)}, f32[13,8,256]{2,1,0:T(8,128)S(1)}, f32[13,8,256]{2,1,0:T(8,128)S(1)}) custom-call(f32[3,2,8,128]{3,2,1,0:T(8,128)S(1)} %collective-permute-done.4.b_near, f32[3,2,8,128]{3,2,1,0:T(8,128)S(1)} %collective-permute-done.5.b_far, ...), custom_call_target="tpu_custom_call" | custom-call | flops 65536 | bytes 1048576 | tf_op jit(solution)/shard_map/pallas_call | solution.py:19
  25.7 0.7 %collective-permute-start.8 = (f32[13,8,256]{2,1,0:T(8,128)S(1)}, f32[13,8,256]{2,1,0:T(8,128)S(1)}, u32[]{:S(2)}, u32[]{:S(2)}) collective-permute-start(f32[13,8,256]{2,1,0:T(8,128)S(1)} %get-tuple-element.63), channel_id=1, source_target_pairs={{0,64},{64,0},{128,192},{192,128},{1,65},{65,1},{129,193},{193,129... | collective-permute-start | bytes 319496 | tf_op jit(solution)/shard_map/ppermute | solution.py:40
  26.5 1.9 %collective-permute-start.9 = (f32[13,8,256]{2,1,0:T(8,128)S(1)}, f32[13,8,256]{2,1,0:T(8,128)S(1)}, u32[]{:S(2)}, u32[]{:S(2)}) collective-permute-start(f32[13,8,256]{2,1,0:T(8,128)S(1)} %get-tuple-element.64), channel_id=1, source_target_pairs={{0,192},{64,128},{128,64},{192,0},{1,193},{65,129},{129,65},{193,1... | collective-permute-start | bytes 319496 | tf_op jit(solution)/shard_map/ppermute | solution.py:39
  28.4 1.9 %shard_map.42 = (f32[64,32,256]{2,1,0:T(8,128)S(1)}, f32[64,32,256]{2,1,0:T(8,128)S(1)}, f32[64,32,128]{2,1,0:T(8,128)S(1)}) custom-call(f32[64,32,256]{2,1,0:T(8,128)S(1)} %get-tuple-element.35.u.refs_0_, f32[64,32,256]{2,1,0:T(8,128)S(1)} %get-tuple-element.49.r.refs_4_, f32[64,32,256]{2,1,0:T(8,128)S(1)} %get-tuple-element.51.s), custom_call_target="tpu_custom_call" | custom-call | flops 10485760 | bytes 1048576 | tf_op jit(solution)/shard_map/pallas_call | solution.py:19
  30.3 7.1 %shard_map.43 = (f32[64,32,256]{2,1,0:T(8,128)}, f32[16,32,256]{2,1,0:T(8,128)S(1)}, f32[4,40,384]{2,1,0:T(8,128)S(1)}, f32[4,40,384]{2,1,0:T(8,128)S(1)}, f32[4,40,384]{2,1,0:T(8,128)S(1)}) custom-call(f32[64,32,256]{2,1,0:T(8,128)S(1)} %get-tuple-element.35.u.refs_0_, f32[64,8,256]{2,1,0:T(8,128)S(1)} %get-tuple-element.38.yu.refs_1_, ...), custom_call_target="tpu_custom_call" | custom-call | flops 31457280 | bytes 1048576 | tf_op jit(solution)/shard_map/pallas_call | solution.py:19
  37.3 0.0 collective-permute-done.6.refs_17_
  37.3 0.0 collective-permute-done.7.refs_18_
  37.3 0.0 collective-permute-done.8.refs_19_
  37.3 0.0 collective-permute-done.9.refs_20_
  37.4 1.9 %shard_map.44 = f32[64,32,256]{2,1,0:T(8,128)} custom-call(f32[64,32,256]{2,1,0:T(8,128)S(1)} %get-tuple-element.35.u.refs_0_, f32[64,8,256]{2,1,0:T(8,128)S(1)} %get-tuple-element.38.yu.refs_1_, f32[64,32,128]{2,1,0:T(8,128)S(1)} %get-tuple-element.41.tu.refs_2_, f32[64,8,128]{2,1,0:T(8,128)S(1)} %get-tuple-element.48.refs_3_, ...), custom_call_target="tpu_custom_call", output_to_operand_aliasing={{}: (12, {})} | custom-call | flops 4194304 | bytes 1048576 | tf_op jit(solution)/shard_map/pallas_call | solution.py:19
  (1 shorter events, 0.0 us)
Async XLA Ops:
  3.3 18.7 %collective-permute-start = (f32[16,5,8,256]{3,2,1,0:T(8,128)S(1)}, f32[16,5,8,256]{3,2,1,0:T(8,128)S(1)}, u32[]{:S(2)}, u32[]{:S(2)}) collective-permute-start(f32[16,5,8,256]{3,2,1,0:T(8,128)S(1)} %get-tuple-element.36), channel_id=1, source_target_pairs={{0,4},{4,0},{8,12},{12,8},{16,20},{20,16},{24,28},{28,24},{32,36},... | collective-permute-start | bytes 1966088 | tf_op jit(solution)/shard_map/ppermute | solution.py:40
  6.6 16.7 %collective-permute-start.1 = (f32[16,5,8,256]{3,2,1,0:T(8,128)S(1)}, f32[16,5,8,256]{3,2,1,0:T(8,128)S(1)}, u32[]{:S(2)}, u32[]{:S(2)}) collective-permute-start(f32[16,5,8,256]{3,2,1,0:T(8,128)S(1)} %get-tuple-element.37), channel_id=1, source_target_pairs={{0,60},{4,8},{8,4},{12,16},{16,12},{20,24},{24,20},{28,32},{32,28}... | collective-permute-start | bytes 1966088 | tf_op jit(solution)/shard_map/ppermute | solution.py:39
  6.6 4.3 %collective-permute-start.2 = (f32[3,2,32,128]{3,2,1,0:T(8,128)S(1)}, f32[3,2,32,128]{3,2,1,0:T(8,128)S(1)}, u32[]{:S(2)}, u32[]{:S(2)}) collective-permute-start(f32[3,2,32,128]{3,2,1,0:T(8,128)S(1)} %get-tuple-element.39), channel_id=1, source_target_pairs={{0,1},{1,0},{2,3},{3,2},{4,5},{5,4},{6,7},{7,6},{8,9},{9,8},{10,11... | collective-permute-start | bytes 294920 | tf_op jit(solution)/shard_map/ppermute | solution.py:40
  7.7 29.6 %collective-permute-start.6 = (f32[10,32,256]{2,1,0:T(8,128)S(1)}, f32[10,32,256]{2,1,0:T(8,128)S(1)}, u32[]{:S(2)}, u32[]{:S(2)}) collective-permute-start(f32[10,32,256]{2,1,0:T(8,128)S(1)} %get-tuple-element.61), channel_id=1, source_target_pairs={{0,64},{64,0},{128,192},{192,128},{1,65},{65,1},{129,193},{193,129... | collective-permute-start | bytes 983048 | tf_op jit(solution)/shard_map/ppermute | solution.py:40
  9.0 28.3 %collective-permute-start.7 = (f32[10,32,256]{2,1,0:T(8,128)S(1)}, f32[10,32,256]{2,1,0:T(8,128)S(1)}, u32[]{:S(2)}, u32[]{:S(2)}) collective-permute-start(f32[10,32,256]{2,1,0:T(8,128)S(1)} %get-tuple-element.62), channel_id=1, source_target_pairs={{0,192},{64,128},{128,64},{192,0},{1,193},{65,129},{129,65},{193,1... | collective-permute-start | bytes 983048 | tf_op jit(solution)/shard_map/ppermute | solution.py:39
  10.9 5.0 %collective-permute-start.3 = (f32[3,2,32,128]{3,2,1,0:T(8,128)S(1)}, f32[3,2,32,128]{3,2,1,0:T(8,128)S(1)}, u32[]{:S(2)}, u32[]{:S(2)}) collective-permute-start(f32[3,2,32,128]{3,2,1,0:T(8,128)S(1)} %get-tuple-element.40), channel_id=1, source_target_pairs={{0,3},{1,2},{2,1},{3,0},{4,7},{5,6},{6,5},{7,4},{8,11},{9,10},{10,... | collective-permute-start | bytes 294920 | tf_op jit(solution)/shard_map/ppermute | solution.py:39
  15.9 7.7 %collective-permute-start.4 = (f32[3,2,8,128]{3,2,1,0:T(8,128)S(1)}, f32[3,2,8,128]{3,2,1,0:T(8,128)S(1)}, u32[]{:S(2)}, u32[]{:S(2)}) collective-permute-start(f32[3,2,8,128]{3,2,1,0:T(8,128)S(1)} %get-tuple-element.42), channel_id=1, source_target_pairs={{0,4},{4,0},{8,12},{12,8},{16,20},{20,16},{24,28},{28,24},{32,36},... | collective-permute-start | bytes 73736 | tf_op jit(solution)/shard_map/ppermute | solution.py:40
  22.0 3.3 %collective-permute-start.5 = (f32[3,2,8,128]{3,2,1,0:T(8,128)S(1)}, f32[3,2,8,128]{3,2,1,0:T(8,128)S(1)}, u32[]{:S(2)}, u32[]{:S(2)}) collective-permute-start(f32[3,2,8,128]{3,2,1,0:T(8,128)S(1)} %get-tuple-element.43), channel_id=1, source_target_pairs={{0,60},{4,8},{8,4},{12,16},{16,12},{20,24},{24,20},{28,32},{32,28}... | collective-permute-start | bytes 73736 | tf_op jit(solution)/shard_map/ppermute | solution.py:39
  25.7 11.6 %collective-permute-start.8 = (f32[13,8,256]{2,1,0:T(8,128)S(1)}, f32[13,8,256]{2,1,0:T(8,128)S(1)}, u32[]{:S(2)}, u32[]{:S(2)}) collective-permute-start(f32[13,8,256]{2,1,0:T(8,128)S(1)} %get-tuple-element.63), channel_id=1, source_target_pairs={{0,64},{64,0},{128,192},{192,128},{1,65},{65,1},{129,193},{193,129... | collective-permute-start | bytes 319496 | tf_op jit(solution)/shard_map/ppermute | solution.py:40
  26.5 10.9 %collective-permute-start.9 = (f32[13,8,256]{2,1,0:T(8,128)S(1)}, f32[13,8,256]{2,1,0:T(8,128)S(1)}, u32[]{:S(2)}, u32[]{:S(2)}) collective-permute-start(f32[13,8,256]{2,1,0:T(8,128)S(1)} %get-tuple-element.64), channel_id=1, source_target_pairs={{0,192},{64,128},{128,64},{192,0},{1,193},{65,129},{129,65},{193,1... | collective-permute-start | bytes 319496 | tf_op jit(solution)/shard_map/ppermute | solution.py:39
